TPU v7x, 32 devices: a whole 2x2x4 slice. The times are simulated.
32 devices in a mesh: tm: 8 (over z, x), trk: 4 (over y, core).
Axes of the slice: x: 2, y: 2, z: 4, core: 2. Of those that a mesh axis runs over, the one named last changes fastest.
Arguments:
- track_embed: bfloat16 [1024, 1024], P(('tm', 'trk')), may hold values from -6 to 6
- view_ids: int32 [1024, 16], P(('tm', 'trk')), may hold values from 0 to 63, all different within a row; in each aligned block of 32 rows (0 to 31, 32 to 63, ...) at most 16 rows name the same one
- view_count: int32 [1024], P(('tm', 'trk')), may hold values from 1 to 16
- key_feats: bfloat16 [8, 8, 512, 1024], P('tm', 'trk'), may hold values from -160 to 160
- value_feats: bfloat16 [8, 8, 512, 1024], P('tm', 'trk'), may hold values from -6 to 6
- track_gain: float32 [1024], replicated, may hold values from 0.5 to 1.5
- w_temporal: bfloat16 [1024, 3072], replicated, may hold values from -0.1875 to 0.1875
- temporal_scale: float32 [8], replicated, may hold values from 0.5 to 40
- w_merge: bfloat16 [1024, 1024], replicated, may hold values from -0.1875 to 0.1875
- box_gain: float32 [1024], replicated, may hold values from 0.5 to 1.5
- w_hidden: bfloat16 [1024, 512], replicated, may hold values from -0.1875 to 0.1875
- b_hidden: float32 [512], replicated, may hold values from -4 to 4
- w_box: bfloat16 [512, 10], replicated, may hold values from -0.25 to 0.25
Outputs:
- refined: bfloat16 [1024, 16, 1024], P(('tm', 'trk'))
- boxes: float32 [1024, 16, 10], P(('tm', 'trk'))
Inputs may be any that keep to these rules, and one draw needn't show every extreme that they name: `view_ids`: entry v stands for frame v // 8 seen by camera v % 8. The 16 entries of one track are distinct. Counting padding entries too, at most 16 of the tracks of one device name any one view, and in some of the devices exactly 16 name one view. Only the first view_count entries of a track's list are visible; the others are padding.
All inputs are finite; a program needn't handle non-finite values.
Results may differ from a plain program's by a relative error of at most 0.0055.
The roundings to bfloat16 on the way count: a program that leaves them out, or rounds other values in their place, can miss the bound.
Values may be sent and summed in bfloat16 or wider, within the bound.
No kernel may reach another device: no remote copies, remote signals or barrier semaphores. Data moves between devices by JAX's collectives and lax.ppermute only.
A program may use at most 64 MiB of HBM per device.

v0:
```python
import math

import jax
import jax.numpy as jnp
from jax import lax
from jax.experimental import pallas as pl
from jax.experimental.pallas import tpu as pltpu
from jax.sharding import PartitionSpec as P

HEADS = 8
CAMS = 8


epsilon = 1e-05
masked_score = -1e30


def from_behind(block, axis, distance):
    devices = range(lax.axis_size(axis))
    route = [((i - distance) % len(devices), i) for i in devices]
    return lax.ppermute(block, axis, route)


def layer_norm(values):
    centre = jnp.mean(values, axis=-1, keepdims=True)
    shifted = values - centre
    spread = jnp.mean(shifted * shifted, axis=-1, keepdims=True)
    return shifted * lax.rsqrt(spread + epsilon)


def time_code(frame_ids, model_width):
    half_width = model_width // 2
    freq_index = jnp.arange(half_width).astype(jnp.float32)
    freq_rates = jnp.exp(freq_index * (-2.0 * math.log(10000.0) / model_width))
    angles = frame_ids.astype(jnp.float32)[..., None] * freq_rates
    return jnp.concatenate([jnp.sin(angles), jnp.cos(angles)], axis=-1)


ROW_BLOCK = 256
HEADS_AT_ONCE = 4


def exchange(block, axis, stride):
    size = lax.axis_size(axis)
    return lax.ppermute(block, axis, [(i, i ^ stride) for i in range(size)])


def gather_tracks(rows, split, sides):
    tm_count = lax.axis_size("tm")
    trk_count = lax.axis_size("trk")
    masks = []
    for axis, size, unit, first in (("tm", tm_count, trk_count, 2), ("trk", trk_count, 1, 4)):
        strides = []
        while first < size:
            strides.append(first)
            masks.append(first * unit)
            first *= 2
        for low in range(0, len(strides), 2):
            group = strides[low : low + 2]
            jumps = group + [sum(group)] * (len(group) - 1)
            rows = jnp.concatenate([rows] + [exchange(rows, axis, jump) for jump in jumps], axis=0)
    rows, sides = lax.optimization_barrier((rows, sides))
    part = rows.shape[0]
    left, right = rows[:, :split], rows[:, split:]
    left_x, right_y = exchange(left, "tm", 1), exchange(right, "trk", 2)
    left = jnp.concatenate([left, left_x], axis=0)
    right = jnp.concatenate([right, right_y], axis=0)
    left_y, right_x = exchange(left, "trk", 2), exchange(right, "tm", 1)
    left = jnp.concatenate([left, left_y], axis=0)
    right = jnp.concatenate([right[:part], right_x[:part], right[part:], right_x[part:]], axis=0)
    masks += [trk_count, 2, 1]
    return left, exchange(left, "trk", 1), right, exchange(right, "trk", 1), masks, sides


def iota(shape, axis):
    return lax.broadcasted_iota(jnp.int32, shape, axis)


def match_row(ids, view):
    hit = jnp.where(ids.astype(jnp.float32) == view, 1.0, 0.0).astype(jnp.bfloat16)
    ones = jnp.ones((8, ids.shape[1]), jnp.bfloat16)
    return lax.dot_general(ones, hit, (((1,), (1,)), ((), ())), preferred_element_type=jnp.float32)


def ranks_of(ids_refs, view, store, width):
    before = iota((width, width), 0) < iota((width, width), 1)
    before = jnp.where(before, 1.0, 0.0).astype(jnp.bfloat16)
    base = jnp.zeros((8, 1), jnp.float32)
    at = 0
    for ids_ref, columns in ids_refs:
        for low in range(0, ids_ref.shape[0], width):
            mask = match_row(ids_ref[low : low + width, columns], view)
            rank = base + jnp.dot(
                mask.astype(jnp.bfloat16), before, preferred_element_type=jnp.float32
            )
            store(at, mask, rank)
            base = base + jnp.sum(mask, axis=1, keepdims=True)
            at += width
    return base


def attend_kernel(
    info_ref,
    left0_ref,
    left1_ref,
    right0_ref,
    right1_ref,
    key0_ref,
    key1_ref,
    value0_ref,
    value1_ref,
    gain_ref,
    code_ref,
    out_ref,
    query_ref,
    rank_ref,
    place_ref,
    pack_ref,
    mixed_ref,
    count_ref,
    *,
    row_block,
    code_width,
    masks,
    block,
    capacity,
):
    head = pl.program_id(0)
    rows_total, step_width = out_ref.shape
    head_width = gain_ref.shape[1] // HEADS
    chunks = rows_total // row_block
    model_width = gain_ref.shape[1]
    half = left0_ref.shape[1] - code_width
    tracks = left0_ref.shape[0]

    @pl.when(head == 0)
    def _():
        view = info_ref[0].astype(jnp.float32)

        width = min(512, tracks)
        inside = (iota((width, width), 0) // block == iota((width, width), 1) // block) & (
            iota((width, width), 0) < iota((width, width), 1)
        )
        inside = jnp.where(inside, 1.0, 0.0).astype(jnp.bfloat16)

        def store(at, mask, rank):
            chosen = mask > 0.5
            here = slice(at, at + width)
            rank_ref[:, here] = jnp.where(chosen, rank, -1.0)
            number = (iota((8, width), 1) + at) // block
            owner = jnp.full((8, width), info_ref[1], jnp.int32)
            for bit, mark in enumerate(masks):
                owner = owner ^ (((number >> bit) & 1) * mark)
            place = jnp.dot(
                mask.astype(jnp.bfloat16), inside, preferred_element_type=jnp.float32
            )
            place = place + owner.astype(jnp.float32) * capacity
            place_ref[:, here] = jnp.where(chosen, place, -1.0)

        columns = slice(half, half + code_width)
        total = ranks_of(((left0_ref, columns), (left1_ref, columns)), view, store, width)
        count_ref[0] = (jnp.max(total).astype(jnp.int32) + row_block - 1) // row_block

        def one_chunk(c, carry):
            wanted = (iota((row_block, 1), 0) + c * row_block).astype(jnp.float32)
            low = jnp.zeros((row_block, half), jnp.float32)
            high = jnp.zeros((row_block, model_width - half), jnp.float32)
            for piece, (left_ref, right_ref) in enumerate(
                ((left0_ref, right0_ref), (left1_ref, right1_ref))
            ):
                ranks = rank_ref[0:1, piece * tracks : (piece + 1) * tracks]
                pick = jnp.where(ranks == wanted, 1.0, 0.0).astype(jnp.bfloat16)
                low += jnp.dot(pick, left_ref[:, :half], preferred_element_type=jnp.float32)
                high += jnp.dot(pick, right_ref[...], preferred_element_type=jnp.float32)
            rows = jnp.concatenate([low, high], axis=1)
            states = layer_norm(rows) * gain_ref[...]
            at = pl.multiple_of(c * row_block, row_block)
            query_ref[pl.ds(at, row_block), :] = (states + code_ref[...]).astype(jnp.bfloat16)
            return carry

        lax.fori_loop(0, count_ref[0], one_chunk, 0)
        mixed_ref[...] = jnp.zeros(mixed_ref.shape, jnp.bfloat16)
        column = (iota((1, rows_total), 1) + 1).astype(jnp.float32)

        def one_stretch(c, carry):
            at = pl.multiple_of(c * row_block, row_block)
            slot = (iota((row_block, 1), 0) + at).astype(jnp.float32)
            hit = place_ref[0:1, :] == slot
            source = jnp.sum(jnp.where(hit, rank_ref[0:1, :] + 1.0, 0.0), axis=1, keepdims=True)
            pick = jnp.where(source == column, 1.0, 0.0)
            pack_ref[pl.ds(at, row_block), :] = pick.astype(jnp.bfloat16)
            return carry

        lax.fori_loop(0, chunks, one_stretch, 0)

    scale = head_width ** (-0.5)
    lane = pl.multiple_of(head * step_width, step_width)
    across = (((1,), (1,)), ((), ()))

    def one_chunk(c, carry):
        at = pl.multiple_of(c * row_block, row_block)
        query = query_ref[pl.ds(at, row_block), pl.ds(lane, step_width)]
        for low in range(0, step_width, head_width):
            own = slice(low, low + head_width)
            scores0 = lax.dot_general(
                query[:, own], key0_ref[:, own], across, preferred_element_type=jnp.float32
            )
            scores1 = lax.dot_general(
                query[:, own], key1_ref[:, own], across, preferred_element_type=jnp.float32
            )
            top = jnp.max(jnp.maximum(scores0, scores1), axis=1, keepdims=True)
            weights0 = jnp.exp((scores0 - top) * scale)
            weights1 = jnp.exp((scores1 - top) * scale)
            totals = jnp.sum(weights0 + weights1, axis=1, keepdims=True)
            mixed = jnp.dot(
                weights0.astype(jnp.bfloat16), value0_ref[:, own], preferred_element_type=jnp.float32
            ) + jnp.dot(
                weights1.astype(jnp.bfloat16), value1_ref[:, own], preferred_element_type=jnp.float32
            )
            mixed_ref[pl.ds(at, row_block), own] = (mixed / totals).astype(jnp.bfloat16)
        return carry

    lax.fori_loop(0, count_ref[0], one_chunk, 0)

    def pack(used):
        out_ref[...] = jnp.dot(
            pack_ref[:, :used], mixed_ref[:used, :], preferred_element_type=jnp.float32
        ).astype(jnp.bfloat16)

    @pl.when(count_ref[0] <= 1)
    def _():
        pack(row_block)

    @pl.when(count_ref[0] > 1)
    def _():
        pack(rows_total)


def attend_view(info, gathered, keys, values, gain, code, capacity, code_width, masks, block):
    left0, _, _, _ = gathered
    model_width = gain.shape[1]
    step_width = model_width // HEADS * HEADS_AT_ONCE
    rows_total = capacity * 2 * left0.shape[0] // block
    row_block = math.gcd(ROW_BLOCK, rows_total)
    whole = lambda a: pl.BlockSpec(a.shape, lambda h: (0,) * a.ndim)

    def part(array, frame, camera):
        return pl.BlockSpec(
            (None, None, array.shape[2], step_width), lambda h: (frame, camera, 0, h)
        )

    tokens = [k for k, _, _ in keys] + [v for v, _, _ in values]
    places = [part(*k) for k in keys] + [part(*v) for v in values]
    return pl.pallas_call(
        lambda *refs: attend_kernel(
            *refs,
            row_block=row_block,
            code_width=code_width,
            masks=masks,
            block=block,
            capacity=capacity,
        ),
        grid=(HEADS // HEADS_AT_ONCE,),
        in_specs=[pl.BlockSpec(memory_space=pltpu.SMEM)]
        + [whole(a) for a in gathered]
        + places
        + [whole(gain), whole(code)],
        out_specs=pl.BlockSpec((rows_total, step_width), lambda h: (0, h)),
        out_shape=jax.ShapeDtypeStruct((rows_total, model_width), jnp.bfloat16),
        scratch_shapes=[
            pltpu.VMEM((rows_total, model_width), jnp.bfloat16),
            pltpu.VMEM((8, 2 * left0.shape[0]), jnp.float32),
            pltpu.VMEM((8, 2 * left0.shape[0]), jnp.float32),
            pltpu.VMEM((rows_total, rows_total), jnp.bfloat16),
            pltpu.VMEM((rows_total, step_width), jnp.bfloat16),
            pltpu.SMEM((1,), jnp.int32),
        ],
        cost_estimate=pl.CostEstimate(
            flops=8 * rows_total * 1024 * model_width, bytes_accessed=1 << 23, transcendentals=0
        ),
        name="attend_view",
    )(info, *gathered, *tokens, gain, code)


def track_block(
    states,
    attended,
    counts,
    w_temporal,
    temporal_scale,
    w_merge,
    box_gain,
    w_hidden,
    b_hidden,
    w_box,
):
    track_rows = states.shape[0]
    list_length = attended.shape[1]
    model_width = states.shape[1]
    head_feature_width = model_width // HEADS
    residual_rows = states[:, None, :] + attended.astype(jnp.float32)
    normed = layer_norm(residual_rows).astype(jnp.bfloat16)
    projected = jnp.dot(
        normed.reshape(track_rows * list_length, model_width),
        w_temporal,
        preferred_element_type=jnp.float32,
    ).astype(jnp.bfloat16)
    projected = projected.reshape(track_rows, list_length, 3, HEADS, head_feature_width)
    per_head_queries = projected[:, :, 0]
    per_head_keys = projected[:, :, 1]
    per_head_values = projected[:, :, 2]
    attention_scores = jnp.einsum(
        "bqhd,bkhd->bhqk", per_head_queries, per_head_keys, preferred_element_type=jnp.float32
    )
    attention_scores = attention_scores * (
        temporal_scale[None, :, None, None] * head_feature_width ** (-0.5)
    )
    positions = jnp.arange(list_length)
    key_valid = positions[None, :] < counts[:, None]
    attention_scores = jnp.where(key_valid[:, None, None, :], attention_scores, masked_score)
    row_top = jnp.max(attention_scores, axis=-1, keepdims=True)
    weights = jnp.exp(attention_scores - row_top)
    probs = (weights / jnp.sum(weights, axis=-1, keepdims=True)).astype(jnp.bfloat16)
    mixed_heads = jnp.einsum(
        "bhqk,bkhd->bqhd", probs, per_head_values, preferred_element_type=jnp.float32
    ).astype(jnp.bfloat16)
    mixed_heads = mixed_heads.reshape(track_rows * list_length, model_width)
    updated = residual_rows + jnp.dot(
        mixed_heads, w_merge, preferred_element_type=jnp.float32
    ).reshape(track_rows, list_length, model_width)
    row_valid = key_valid.astype(jnp.float32)[:, :, None]
    refined = (updated * row_valid).astype(jnp.bfloat16)
    box_input = (layer_norm(updated) * box_gain).astype(jnp.bfloat16)
    box_hidden = jax.nn.gelu(
        jnp.dot(
            box_input.reshape(track_rows * list_length, model_width),
            w_hidden,
            preferred_element_type=jnp.float32,
        )
        + b_hidden
    ).astype(jnp.bfloat16)
    box_values = (
        jnp.dot(box_hidden, w_box, preferred_element_type=jnp.float32).reshape(
            track_rows, list_length, w_box.shape[1]
        )
        * row_valid
    )
    return (refined, box_values)


def local(
    track_embed,
    view_ids,
    view_count,
    key_feats,
    value_feats,
    track_gain,
    w_temporal,
    temporal_scale,
    w_merge,
    box_gain,
    w_hidden,
    b_hidden,
    w_box,
):
    tm_count = lax.axis_size("tm")
    trk_count = lax.axis_size("trk")
    device_count = tm_count * trk_count
    device = lax.axis_index("tm") * trk_count + lax.axis_index("trk")
    local_frames = key_feats.shape[0]
    local_cameras = key_feats.shape[1]
    model_width = track_embed.shape[1]
    track_local = track_embed.shape[0]
    list_length = view_ids.shape[1]
    row_local = track_local * list_length
    view_total = local_frames * tm_count * CAMS
    capacity = max(2, (2 * row_local + view_total - 1) // view_total)
    local_views = local_frames * local_cameras
    code_width = 128

    valid = jnp.arange(list_length)[None, :] < view_count[:, None]
    frames = view_ids // CAMS
    cameras = view_ids % CAMS
    owner = frames // local_frames * trk_count + cameras // local_cameras
    ordered_view = owner * local_views + frames % local_frames * local_cameras
    ordered_view = ordered_view + cameras % local_cameras
    listed = jnp.where(valid, ordered_view, -1)

    tagged = jnp.pad(
        listed.astype(jnp.bfloat16), ((0, 0), (0, code_width - list_length)), constant_values=-1
    )
    half = model_width // 2
    tagged = jnp.concatenate([track_embed[:, :half], tagged, track_embed[:, half:]], axis=1)
    left0, left1, right0, right1, masks, firsts = gather_tracks(
        tagged, half + code_width, (key_feats[:, :1], value_feats[:, :1])
    )
    next_key = from_behind(firsts[0], "trk", -1)
    next_value = from_behind(firsts[1], "trk", -1)

    gain = track_gain.reshape(1, model_width)
    gathered = (left0, left1, right0, right1)
    returned = []
    first_view = device * local_views
    for frame in range(local_frames):
        frame_id = lax.axis_index("tm") * local_frames + frame
        code = time_code(frame_id.reshape(1), model_width)
        for camera in range(local_cameras):
            following = camera + 1
            if following < local_cameras:
                keys = [(key_feats, frame, camera), (key_feats, frame, following)]
                values = [(value_feats, frame, camera), (value_feats, frame, following)]
            else:
                keys = [(key_feats, frame, camera), (next_key, frame, 0)]
                values = [(value_feats, frame, camera), (next_value, frame, 0)]
            info = jnp.stack([first_view + len(returned), device]).astype(jnp.int32)
            outbound = attend_view(
                info, gathered, keys, values, gain, code, capacity, code_width, masks, track_local
            )
            outbound, first_view = lax.optimization_barrier((outbound, first_view))
            returned.append(
                lax.all_to_all(
                    outbound.reshape(device_count, capacity, model_width),
                    ("tm", "trk"),
                    split_axis=0,
                    concat_axis=0,
                    tiled=True,
                )
            )

    flat = listed.reshape(row_local)
    index = jnp.arange(row_local, dtype=jnp.int32)
    ahead = (flat[None, :] == flat[:, None]) & (index[None, :] < index[:, None])
    place = flat // local_views * capacity + jnp.sum(ahead.astype(jnp.int32), axis=1)
    slots = device_count * capacity
    attended = jnp.zeros((row_local, model_width), jnp.float32)
    for view, arrived in enumerate(returned):
        wanted = jnp.where((flat >= 0) & (flat % local_views == view), place, -1)
        pick = (wanted[:, None] == jnp.arange(slots)[None, :]).astype(jnp.bfloat16)
        attended += jnp.dot(
            pick, arrived.reshape(slots, model_width), preferred_element_type=jnp.float32
        )
    attended = attended.reshape(track_local, list_length, model_width)
    states = layer_norm(track_embed.astype(jnp.float32)) * track_gain
    return track_block(
        states,
        attended,
        view_count,
        w_temporal,
        temporal_scale,
        w_merge,
        box_gain,
        w_hidden,
        b_hidden,
        w_box,
    )


def solution(mesh):
    placed = (
        P(("tm", "trk"), None),
        P(("tm", "trk"), None),
        P(("tm", "trk")),
        P("tm", "trk", None, None),
        P("tm", "trk", None, None),
        P(),
        P(),
        P(),
        P(),
        P(),
        P(),
        P(),
        P(),
    )
    return jax.shard_map(
        local,
        mesh=mesh,
        in_specs=placed,
        out_specs=(P(("tm", "trk"), None, None), P(("tm", "trk"), None, None)),
        check_vma=False,
    )
```

profile of v0, /device:TPU:0, one launch (start us, length us, event | category | flops | bytes accessed | tf_op | source)
XLA Modules:
  0.0 154.2 jit_solution(10444875800552581489)
XLA Ops:
  0.6 0.0 copy-start
  0.6 0.9 fusion.65
  1.6 0.8 copy.35
  2.3 0.9 fusion.61
  3.3 3.1 %collective-permute-start = (bf16[32,1152]{1,0:T(8,128)(2,1)S(1)}, bf16[32,1152]{1,0:T(8,128)(2,1)S(1)}, u32[]{:S(2)}, u32[]{:S(2)}) collective-permute-start(bf16[32,1152]{1,0:T(8,128)(2,1)S(1)} %pad_maximum_fusion.5), channel_id=1, source_target_pairs={{0,8},{4,12},{8,0},{12,4},{16,24},{20,28},{24,16},{28,20},{1,9},{5... | collective-permute-start | bytes 221192 | tf_op jit(solution)/shard_map/ppermute | solution.py:45
  6.4 2.6 %collective-permute-start.1 = (bf16[32,1152]{1,0:T(8,128)(2,1)S(1)}, bf16[32,1152]{1,0:T(8,128)(2,1)S(1)}, u32[]{:S(2)}, u32[]{:S(2)}) collective-permute-start(bf16[32,1152]{1,0:T(8,128)(2,1)S(1)} %pad_maximum_fusion.5), channel_id=1, source_target_pairs={{0,16},{4,20},{8,24},{12,28},{16,0},{20,4},{24,8},{28,12},{1,17},{... | collective-permute-start | bytes 221192 | tf_op jit(solution)/shard_map/ppermute | solution.py:45
  9.0 0.0 collective-permute-start.2
  9.0 2.3 %slice.35 = bf16[1,1,512,1024]{3,2,1,0:T(8,128)(2,1)} slice(bf16[1,2,512,1024]{3,2,1,0:T(8,128)(2,1)} %refs_5_.3), slice={[0:1], [0:1], [0:512], [0:1024]} | slice | bytes 2097152 | tf_op jit(solution)/shard_map/slice | solution.py:395
  11.2 1.0 slice.36
  12.3 0.0 collective-permute-done
  12.3 1.9 %collective-permute-done.1 = bf16[32,1152]{1,0:T(8,128)(2,1)S(1)} collective-permute-done((bf16[32,1152]{1,0:T(8,128)(2,1)S(1)}, bf16[32,1152]{1,0:T(8,128)(2,1)S(1)}, u32[]{:S(2)}, u32[]{:S(2)}) %collective-permute-start.1) | collective-permute-done | bytes 73760 | tf_op jit(solution)/shard_map/ppermute | solution.py:45
  14.2 1.1 collective-permute-done.2
  15.3 1.6 %collective-permute-start.3 = (bf16[128,640]{1,0:T(8,128)(2,1)S(1)}, bf16[128,640]{1,0:T(8,128)(2,1)S(1)}, u32[]{:S(2)}, u32[]{:S(2)}) collective-permute-start(bf16[128,640]{1,0:T(8,128)(2,1)S(1)} %slice.37), channel_id=1, source_target_pairs={{0,4},{4,0},{8,12},{12,8},{16,20},{20,16},{24,28},{28,24},{1,5},{5... | collective-permute-start | bytes 491528 | tf_op jit(solution)/shard_map/ppermute | solution.py:45
  16.8 1.6 %collective-permute-start.6 = (bf16[128,512]{1,0:T(8,128)(2,1)S(1)}, bf16[128,512]{1,0:T(8,128)(2,1)S(1)}, u32[]{:S(2)}, u32[]{:S(2)}) collective-permute-start(bf16[128,512]{1,0:T(8,128)(2,1)S(1)} %slice.38), channel_id=1, source_target_pairs={{0,2},{1,3},{2,0},{3,1},{4,6},{5,7},{6,4},{7,5},{8,10},{9,11},{10,... | collective-permute-start | bytes 393224 | tf_op jit(solution)/shard_map/ppermute | solution.py:45
  18.4 2.2 %collective-permute-done.3 = bf16[128,640]{1,0:T(8,128)(2,1)S(1)} collective-permute-done((bf16[128,640]{1,0:T(8,128)(2,1)S(1)}, bf16[128,640]{1,0:T(8,128)(2,1)S(1)}, u32[]{:S(2)}, u32[]{:S(2)}) %collective-permute-start.3) | collective-permute-done | bytes 163872 | tf_op jit(solution)/shard_map/ppermute | solution.py:45
  20.7 1.6 %collective-permute-start.4 = (bf16[256,640]{1,0:T(8,128)(2,1)S(1)}, bf16[256,640]{1,0:T(8,128)(2,1)S(1)}, u32[]{:S(2)}, u32[]{:S(2)}) collective-permute-start(bf16[256,640]{1,0:T(8,128)(2,1)S(1)} %pad_maximum_fusion.2), channel_id=1, source_target_pairs={{0,2},{1,3},{2,0},{3,1},{4,6},{5,7},{6,4},{7,5},{8,10},{9,11},{10,... | collective-permute-start | bytes 983048 | tf_op jit(solution)/shard_map/ppermute | solution.py:45
  22.3 1.0 collective-permute-done.6
  23.3 0.7 collective-permute-start.7
  24.0 4.7 %collective-permute-done.4 = bf16[256,640]{1,0:T(8,128)(2,1)S(1)} collective-permute-done((bf16[256,640]{1,0:T(8,128)(2,1)S(1)}, bf16[256,640]{1,0:T(8,128)(2,1)S(1)}, u32[]{:S(2)}, u32[]{:S(2)}) %collective-permute-start.4) | collective-permute-done | bytes 327712 | tf_op jit(solution)/shard_map/ppermute | solution.py:45
  28.6 0.1 pad_maximum_fusion.refs_1_
  28.7 0.1 collective-permute-start.5
  28.8 0.9 collective-permute-done.7
  29.8 0.1 collective-permute-start.8
  29.9 0.6 pad_add_fusion.refs_0_
  30.5 0.1 fusion.54
  30.6 0.6 pad_maximum_fusion.6.refs_10_
  31.2 0.7 collective-permute-done.8.refs_4_
  31.9 0.0 collective-permute-done.5.refs_2_
  31.9 10.2 %attend_view.2 = bf16[512,1024]{1,0:T(8,128)(2,1)} custom-call(s32[2]{0:T(128)} %pad_add_fusion.refs_0_, bf16[512,640]{1,0:T(8,128)(2,1)} %copy-done.4, bf16[512,640]{1,0:T(8,128)(2,1)} %collective-permute-done.5.refs_2_, bf16[512,512]{1,0:T(8,128)(2,1)} %copy-done.6, bf16[512,512]{1,0:T(8,128)(2,1)} %collective-permute-done.8.refs_4_, ...), custom_call_target="tpu_custom_call" | custom-call | flops 4294967296 | bytes 8388608 | tf_op jit(solution)/shard_map/attend_view/pallas_call | solution.py:254
  42.1 4.0 %all-to-all-start = ((bf16[32,16,1024]{2,1,0:T(8,128)(2,1)}), bf16[32,16,1024]{2,1,0:T(8,128)(2,1)S(1)}, u32[]{:S(2)}, u32[]{:S(2)}) async-start(bf16[32,16,1024]{2,1,0:T(8,128)(2,1)} %bitcast.69), calls=%async_computation | async-start | bytes 2097152 | tf_op jit(solution)/shard_map/all_to_all | solution.py:421
  46.0 1.5 collective-permute-start.10
  47.6 0.4 collective-permute-start.9
  48.0 0.1 reshape.247
  48.1 0.1 convert_reduce_fusion.1
  48.2 0.7 pad_add_fusion.1.refs_0_
  48.8 19.4 %collective-permute-done.10.refs_8_ = bf16[1,1,512,1024]{3,2,1,0:T(8,128)(2,1)} collective-permute-done((bf16[1,1,512,1024]{3,2,1,0:T(8,128)(2,1)}, bf16[1,1,512,1024]{3,2,1,0:T(8,128)(2,1)}, u32[]{:S(2)}, u32[]{:S(2)}) %collective-permute-start.10) | collective-permute-done | bytes 1048608 | tf_op jit(solution)/shard_map/ppermute | solution.py:21
  68.3 12.6 %collective-permute-done.9.refs_6_ = bf16[1,1,512,1024]{3,2,1,0:T(8,128)(2,1)} collective-permute-done((bf16[1,1,512,1024]{3,2,1,0:T(8,128)(2,1)}, bf16[1,1,512,1024]{3,2,1,0:T(8,128)(2,1)}, u32[]{:S(2)}, u32[]{:S(2)}) %collective-permute-start.9) | collective-permute-done | bytes 1048608 | tf_op jit(solution)/shard_map/ppermute | solution.py:21
  80.8 10.2 %attend_view.3 = bf16[512,1024]{1,0:T(8,128)(2,1)} custom-call(s32[2]{0:T(128)} %pad_add_fusion.1.refs_0_, bf16[512,640]{1,0:T(8,128)(2,1)} %copy-done.4, bf16[512,640]{1,0:T(8,128)(2,1)} %collective-permute-done.5.refs_2_, bf16[512,512]{1,0:T(8,128)(2,1)} %copy-done.6, bf16[512,512]{1,0:T(8,128)(2,1)} %collective-permute-done.8.refs_4_, ...), custom_call_target="tpu_custom_call" | custom-call | flops 4294967296 | bytes 8388608 | tf_op jit(solution)/shard_map/attend_view/pallas_call | solution.py:254
  91.0 0.0 copy-start.9
  91.1 0.0 copy-start.8
  91.1 9.8 %all-to-all-start.1 = ((bf16[32,16,1024]{2,1,0:T(8,128)(2,1)}), bf16[32,16,1024]{2,1,0:T(8,128)(2,1)}, u32[]{:S(2)}, u32[]{:S(2)}) async-start(bf16[32,16,1024]{2,1,0:T(8,128)(2,1)} %bitcast.70), calls=%async_computation.1 | async-start | bytes 2097152 | tf_op jit(solution)/shard_map/all_to_all | solution.py:421
  100.9 0.2 fusion.37
  101.1 0.2 convert_reduce_fusion
  101.4 0.1 fusion.50
  101.5 0.1 fusion.38
  101.6 2.1 %fusion.26 = f32[512,1024]{1,0:T(8,128)} fusion(bf16[512,1024]{1,0:T(8,128)(2,1)S(1)} %bitcast.67, s32[512]{0:T(512)S(1)} %and_select_fusion.1), kind=kOutput, calls=%fused_computation.46 | convolution fusion | flops 537133056 | bytes 3147776 | tf_op jit(solution)/shard_map/dot_general | solution.py:439
  103.7 23.2 %all-to-all-done.1 = bf16[32,16,1024]{2,1,0:T(8,128)(2,1)} async-done(((bf16[32,16,1024]{2,1,0:T(8,128)(2,1)}), bf16[32,16,1024]{2,1,0:T(8,128)(2,1)}, u32[]{:S(2)}, u32[]{:S(2)}) %all-to-all-start.1) | async-done | bytes 1048608 | tf_op jit(solution)/shard_map/all_to_all | solution.py:421
  126.9 2.8 %fusion.4 = (f32[512]{0:T(512)S(1)}, f32[512,1024]{1,0:T(8,128)S(1)}) fusion(f32[32,1024]{1,0:T(8,128)S(1)} %fusion.38, f32[512,1024]{1,0:T(8,128)} %fusion.26, bf16[512,1024]{1,0:T(8,128)(2,1)} %bitcast.7, s32[512]{0:T(512)S(1)} %get-tuple-element.18), kind=kOutput, calls=%fused_computation.15 | convolution fusion | flops 538705408 | bytes 5378048 | tf_op jit(solution)/shard_map/dot_general | solution.py:439
  129.7 0.4 multiply_reduce_fusion.1
  130.1 0.9 copy-done.1
  131.0 0.4 multiply_convert_fusion.2
  131.4 6.4 %fusion.5 = bf16[64,8,24,128]{3,1,2,0:T(8,128)(2,1)S(1)} fusion(bf16[512,1024]{1,0:T(8,128)(2,1)S(1)} %multiply_convert_fusion.2, bf16[1024,3072]{1,0:T(8,128)(2,1)} %param.19), kind=kOutput, calls=%fused_computation.16 | convolution fusion | flops 3222798336 | bytes 10485760 | tf_op jit(solution)/shard_map/dot_general | solution.py:303
  137.8 0.9 copy.50
  138.7 2.3 %fusion.63 = (bf16[32,16,1,8,128]{4,3,2,1,0:T(8,128)(2,1)S(1)}, bf16[32,16,1,8,128]{4,3,2,1,0:T(8,128)(2,1)}, bf16[32,16,1,8,128]{4,3,2,1,0:T(8,128)(2,1)}) fusion(bf16[32,16,3,8,128]{4,3,2,1,0:T(8,128)(2,1)S(1)} %bitcast.66), kind=kLoop, calls=%fused_computation.125 | loop fusion | bytes 6291456 | tf_op jit(solution)/shard_map/slice | solution.py:311
  141.0 4.1 %fusion.66 = (f32[32,8,16]{2,1,0:T(8,128)S(1)}, f32[32,8,16,16]{2,3,1,0:T(8,128)}) fusion(f32[8]{0:T(128)S(1)} %broadcast_multiply_fusion.3, pred[32,16]{1,0:T(8,128)(4,1)S(1)} %get-tuple-element.32, bf16[32,16,1,8,128]{4,3,2,1,0:T(8,128)(2,1)} %get-tuple-element.24, bf16[32,16,1,8,128]{4,3,2,1,0:T(8,128)(2,1)} %get-tuple-element.23), kind=kOutput, calls=%fused_computation.128 | convolution fusion | flops 17039376 | bytes 2376224 | tf_op jit(solution)/shard_map/sub | solution.py:322
  145.1 2.3 %fusion.9 = bf16[32,8,2,8,128]{4,3,2,1,0:T(8,128)(2,1)S(1)} fusion(f32[32,8,16,16]{2,3,1,0:T(8,128)} %get-tuple-element.36, bf16[32,16,1,8,128]{4,3,2,1,0:T(8,128)(2,1)S(1)} %get-tuple-element.22, f32[32,8,16]{2,1,0:T(8,128)S(1)} %get-tuple-element.35), kind=kOutput, calls=%fused_computation.21 | convolution fusion | flops 17432576 | bytes 2375680 | tf_op jit(solution)/shard_map/bhqk,bkhd->bqhd/dot_general | solution.py:324
  147.4 1.4 fusion.67
  148.8 0.0 copy-start.7
  148.8 0.3 multiply_reduce_fusion
  149.2 0.3 copy-done.7
  149.5 1.4 multiply_convert_fusion
  150.9 2.3 %fusion.18 = f32[512,10]{0,1:T(8,128)S(1)} fusion(bf16[512,10]{0,1:T(8,128)(2,1)S(1)} %copy-done.10, bf16[512,1024]{1,0:T(8,128)(2,1)S(1)} %bitcast.68, bf16[1024,512]{1,0:T(8,128)(2,1)} %param.23, f32[512]{0:T(512)S(1)} %copy-done.11), kind=kOutput, calls=%fused_computation.31 | convolution fusion | flops 544735232 | bytes 2129920 | tf_op jit(solution)/shard_map/dot_general | solution.py:343
  153.3 0.1 reshape.255
  153.4 0.7 copy.44
  (40 shorter events, 0.3 us)
Async XLA Ops:
  0.6 146.7 %copy-start = (bf16[1024,1024]{1,0:T(8,128)(2,1)S(1)}, bf16[1024,1024]{1,0:T(8,128)(2,1)}, u32[]{:S(2)}) copy-start(bf16[1024,1024]{1,0:T(8,128)(2,1)} %param.21) | copy-start | bytes 6291460
  2.3 8.9 %copy-start.5 = (bf16[1,2,512,1024]{3,2,1,0:T(8,128)(2,1)S(1)}, bf16[1,2,512,1024]{3,2,1,0:T(8,128)(2,1)}, u32[]{:S(2)}) copy-start(bf16[1,2,512,1024]{3,2,1,0:T(8,128)(2,1)} %refs_7_.3) | copy-start | bytes 6291460
  3.3 9.0 %collective-permute-start = (bf16[32,1152]{1,0:T(8,128)(2,1)S(1)}, bf16[32,1152]{1,0:T(8,128)(2,1)S(1)}, u32[]{:S(2)}, u32[]{:S(2)}) collective-permute-start(bf16[32,1152]{1,0:T(8,128)(2,1)S(1)} %pad_maximum_fusion.5), channel_id=1, source_target_pairs={{0,8},{4,12},{8,0},{12,4},{16,24},{20,28},{24,16},{28,20},{1,9},{5... | collective-permute-start | bytes 221192 | tf_op jit(solution)/shard_map/ppermute | solution.py:45
  6.4 7.8 %collective-permute-start.1 = (bf16[32,1152]{1,0:T(8,128)(2,1)S(1)}, bf16[32,1152]{1,0:T(8,128)(2,1)S(1)}, u32[]{:S(2)}, u32[]{:S(2)}) collective-permute-start(bf16[32,1152]{1,0:T(8,128)(2,1)S(1)} %pad_maximum_fusion.5), channel_id=1, source_target_pairs={{0,16},{4,20},{8,24},{12,28},{16,0},{20,4},{24,8},{28,12},{1,17},{... | collective-permute-start | bytes 221192 | tf_op jit(solution)/shard_map/ppermute | solution.py:45
  9.0 6.3 %collective-permute-start.2 = (bf16[32,1152]{1,0:T(8,128)(2,1)S(1)}, bf16[32,1152]{1,0:T(8,128)(2,1)S(1)}, u32[]{:S(2)}, u32[]{:S(2)}) collective-permute-start(bf16[32,1152]{1,0:T(8,128)(2,1)S(1)} %pad_maximum_fusion.5), channel_id=1, source_target_pairs={{0,24},{4,28},{8,16},{12,20},{16,8},{20,12},{24,0},{28,4},{1,25},{... | collective-permute-start | bytes 221192 | tf_op jit(solution)/shard_map/ppermute | solution.py:45
  15.3 5.4 %collective-permute-start.3 = (bf16[128,640]{1,0:T(8,128)(2,1)S(1)}, bf16[128,640]{1,0:T(8,128)(2,1)S(1)}, u32[]{:S(2)}, u32[]{:S(2)}) collective-permute-start(bf16[128,640]{1,0:T(8,128)(2,1)S(1)} %slice.37), channel_id=1, source_target_pairs={{0,4},{4,0},{8,12},{12,8},{16,20},{20,16},{24,28},{28,24},{1,5},{5... | collective-permute-start | bytes 491528 | tf_op jit(solution)/shard_map/ppermute | solution.py:45
  16.8 6.4 %collective-permute-start.6 = (bf16[128,512]{1,0:T(8,128)(2,1)S(1)}, bf16[128,512]{1,0:T(8,128)(2,1)S(1)}, u32[]{:S(2)}, u32[]{:S(2)}) collective-permute-start(bf16[128,512]{1,0:T(8,128)(2,1)S(1)} %slice.38), channel_id=1, source_target_pairs={{0,2},{1,3},{2,0},{3,1},{4,6},{5,7},{6,4},{7,5},{8,10},{9,11},{10,... | collective-permute-start | bytes 393224 | tf_op jit(solution)/shard_map/ppermute | solution.py:45
  20.7 8.0 %collective-permute-start.4 = (bf16[256,640]{1,0:T(8,128)(2,1)S(1)}, bf16[256,640]{1,0:T(8,128)(2,1)S(1)}, u32[]{:S(2)}, u32[]{:S(2)}) collective-permute-start(bf16[256,640]{1,0:T(8,128)(2,1)S(1)} %pad_maximum_fusion.2), channel_id=1, source_target_pairs={{0,2},{1,3},{2,0},{3,1},{4,6},{5,7},{6,4},{7,5},{8,10},{9,11},{10,... | collective-permute-start | bytes 983048 | tf_op jit(solution)/shard_map/ppermute | solution.py:45
  23.3 6.4 %collective-permute-start.7 = (bf16[256,512]{1,0:T(8,128)(2,1)S(1)}, bf16[256,512]{1,0:T(8,128)(2,1)S(1)}, u32[]{:S(2)}, u32[]{:S(2)}) collective-permute-start(bf16[256,512]{1,0:T(8,128)(2,1)S(1)} %pad_maximum_fusion.4), channel_id=1, source_target_pairs={{0,4},{4,0},{8,12},{12,8},{16,20},{20,16},{24,28},{28,24},{1,5},{5... | collective-permute-start | bytes 786440 | tf_op jit(solution)/shard_map/ppermute | solution.py:45
  28.7 3.2 %copy-start.4 = (bf16[512,640]{1,0:T(8,128)(2,1)}, bf16[512,640]{1,0:T(8,128)(2,1)S(1)}, u32[]{:S(2)}) copy-start(bf16[512,640]{1,0:T(8,128)(2,1)S(1)} %pad_maximum_fusion.refs_1_) | copy-start | bytes 1966084
  28.7 3.2 %collective-permute-start.5 = (bf16[512,640]{1,0:T(8,128)(2,1)S(1)}, bf16[512,640]{1,0:T(8,128)(2,1)}, u32[]{:S(2)}, u32[]{:S(2)}) collective-permute-start(bf16[512,640]{1,0:T(8,128)(2,1)S(1)} %pad_maximum_fusion.refs_1_), channel_id=1, source_target_pairs={{0,1},{1,0},{2,3},{3,2},{4,5},{5,4},{6,7},{7,6},{8,9},{9,8},{10,11... | collective-permute-start | bytes 1966088 | tf_op jit(solution)/shard_map/ppermute | solution.py:45
  29.8 2.1 %copy-start.6 = (bf16[512,512]{1,0:T(8,128)(2,1)}, bf16[512,512]{1,0:T(8,128)(2,1)S(1)}, u32[]{:S(2)}) copy-start(bf16[512,512]{1,0:T(8,128)(2,1)S(1)} %pad_maximum_fusion.1.refs_3_) | copy-start | bytes 1572868
  29.8 2.1 %collective-permute-start.8 = (bf16[512,512]{1,0:T(8,128)(2,1)S(1)}, bf16[512,512]{1,0:T(8,128)(2,1)}, u32[]{:S(2)}, u32[]{:S(2)}) collective-permute-start(bf16[512,512]{1,0:T(8,128)(2,1)S(1)} %pad_maximum_fusion.1.refs_3_), channel_id=1, source_target_pairs={{0,1},{1,0},{2,3},{3,2},{4,5},{5,4},{6,7},{7,6},{8,9},{9,8},{10,11... | collective-permute-start | bytes 1572872 | tf_op jit(solution)/shard_map/ppermute | solution.py:45
  42.1 6.0 %copy-start.3 = (bf16[32,1024]{1,0:T(8,128)(2,1)S(1)}, bf16[32,1024]{1,0:T(8,128)(2,1)}, u32[]{:S(2)}) copy-start(bf16[32,1024]{1,0:T(8,128)(2,1)} %param.13) | copy-start | bytes 196612
  42.1 49.0 %all-to-all-start = ((bf16[32,16,1024]{2,1,0:T(8,128)(2,1)}), bf16[32,16,1024]{2,1,0:T(8,128)(2,1)S(1)}, u32[]{:S(2)}, u32[]{:S(2)}) async-start(bf16[32,16,1024]{2,1,0:T(8,128)(2,1)} %bitcast.69), calls=%async_computation | async-start | bytes 2097152 | tf_op jit(solution)/shard_map/all_to_all | solution.py:421
  46.0 22.2 %collective-permute-start.10 = (bf16[1,1,512,1024]{3,2,1,0:T(8,128)(2,1)}, bf16[1,1,512,1024]{3,2,1,0:T(8,128)(2,1)}, u32[]{:S(2)}, u32[]{:S(2)}) collective-permute-start(bf16[1,1,512,1024]{3,2,1,0:T(8,128)(2,1)} %slice.36), channel_id=1, source_target_pairs={{1,0},{2,1},{3,2},{0,3},{5,4},{6,5},{7,6},{4,7},{9,8},{10,9},{11,1... | collective-permute-start | bytes 3145736 | tf_op jit(solution)/shard_map/ppermute | solution.py:21
  47.6 33.2 %collective-permute-start.9 = (bf16[1,1,512,1024]{3,2,1,0:T(8,128)(2,1)}, bf16[1,1,512,1024]{3,2,1,0:T(8,128)(2,1)}, u32[]{:S(2)}, u32[]{:S(2)}) collective-permute-start(bf16[1,1,512,1024]{3,2,1,0:T(8,128)(2,1)} %slice.35), channel_id=1, source_target_pairs={{1,0},{2,1},{3,2},{0,3},{5,4},{6,5},{7,6},{4,7},{9,8},{10,9},{11,1... | collective-permute-start | bytes 3145736 | tf_op jit(solution)/shard_map/ppermute | solution.py:21
  91.0 10.3 %copy-start.12 = (f32[8]{0:T(128)S(1)}, f32[8]{0:T(128)}, u32[]{:S(2)}) copy-start(f32[8]{0:T(128)} %param.20) | copy-start | bytes 100
  91.0 10.4 %copy-start.9 = (s32[32]{0:T(128)S(1)}, s32[32]{0:T(128)}, u32[]{:S(2)}) copy-start(s32[32]{0:T(128)} %param.15) | copy-start | bytes 388
  91.1 10.5 %copy-start.8 = (f32[1024]{0:T(1024)S(1)}, f32[1024]{0:T(1024)}, u32[]{:S(2)}) copy-start(f32[1024]{0:T(1024)} %param.18) | copy-start | bytes 12292
  91.1 35.8 %all-to-all-start.1 = ((bf16[32,16,1024]{2,1,0:T(8,128)(2,1)}), bf16[32,16,1024]{2,1,0:T(8,128)(2,1)}, u32[]{:S(2)}, u32[]{:S(2)}) async-start(bf16[32,16,1024]{2,1,0:T(8,128)(2,1)} %bitcast.70), calls=%async_computation.1 | async-start | bytes 2097152 | tf_op jit(solution)/shard_map/all_to_all | solution.py:421
  129.7 1.3 copy-start.1
  145.1 2.3 %copy-start.2 = (f32[512,1024]{1,0:T(8,128)S(1)}, f32[512,1024]{1,0:T(8,128)}, u32[]{:S(2)}) copy-start(f32[512,1024]{1,0:T(8,128)} %copy-done.1) | copy-start | bytes 6291460
  148.8 0.7 copy-start.7
  149.5 1.4 copy-start.10
  149.5 1.4 copy-start.11
where the time goes:
time: 155 us; the launch traced here: 154 us
  waiting for transfers between devices  67.7 us (44%)
  starting transfers between devices  27 us (17%)
  matrix products  21.4 us (14%)
  Pallas kernels  20.4 us (13%)
  local copies, waits for them, and re-layouts  10.4 us (7%)
  other arithmetic  6.39 us (4%)
    ppermute x2, waiting for transfers between devices, from_behind(): return lax.ppermute(block, axis, route)  32 us
    all_to_all x2, waiting for transfers between devices, local(): lax.all_to_all(outbound.reshape(device_count, capacity, model_width), ('t...  23.2 us
    pallas_call x2, Pallas kernels, attend_view(): pl.pallas_call(lambda *refs: attend_kernel(*refs, row_block=row_block, co...  20.4 us
    all_to_all x2, starting transfers between devices, local(): lax.all_to_all(outbound.reshape(device_count, capacity, model_width), ('t...  13.8 us
    ppermute x9, waiting for transfers between devices, exchange(): return lax.ppermute(block, axis, [(i, i ^ stride) for i in range(size)])  12.5 us
    ppermute x9, starting transfers between devices, exchange(): return lax.ppermute(block, axis, [(i, i ^ stride) for i in range(size)])  11.2 us
    dot_general x1, matrix products, track_block(): jnp.dot(normed.reshape(track_rows * list_length, model_width), w_temporal...  6.45 us
    dot_general x2, matrix products, local(): jnp.dot(pick, arrived.reshape(slots, model_width), preferred_element_type...  4.84 us
  transfers between devices with their start and end apart: 13, of which 10 were waited for; matrix products, arithmetic and copies ran while one was open for 5% of the time, Pallas kernels for 7%

commit v1 on v0

--- a/solution.py
+++ b/solution.py
@@ -38,6 +38,7 @@
 
 ROW_BLOCK = 256
 HEADS_AT_ONCE = 4
+TRACK_BLOCK = 32
 
 
 def exchange(block, axis, stride):
@@ -231,7 +232,11 @@
     def _():
         pack(row_block)
 
-    @pl.when(count_ref[0] > 1)
+    @pl.when(count_ref[0] == 2)
+    def _():
+        pack(min(2 * row_block, rows_total))
+
+    @pl.when(count_ref[0] > 2)
     def _():
         pack(rows_total)
 
@@ -282,70 +287,137 @@
     )(info, *gathered, *tokens, gain, code)
 
 
-def track_block(
-    states,
-    attended,
-    counts,
-    w_temporal,
-    temporal_scale,
-    w_merge,
-    box_gain,
-    w_hidden,
-    b_hidden,
-    w_box,
+def track_kernel(
+    *refs,
+    views,
+    list_length,
 ):
-    track_rows = states.shape[0]
-    list_length = attended.shape[1]
-    model_width = states.shape[1]
-    head_feature_width = model_width // HEADS
-    residual_rows = states[:, None, :] + attended.astype(jnp.float32)
-    normed = layer_norm(residual_rows).astype(jnp.bfloat16)
+    (
+        scale_ref,
+        states_ref,
+        place_ref,
+        counts_ref,
+        key_counts_ref,
+    ) = refs[:5]
+    arrived = refs[5 : 5 + views]
+    (
+        w_temporal_ref,
+        w_merge_ref,
+        box_gain_ref,
+        w_hidden_ref,
+        b_hidden_ref,
+        w_box_ref,
+        refined_ref,
+        boxes_ref,
+        mixed_ref,
+    ) = refs[5 + views :]
+    rows, model_width = refined_ref.shape
+    head_width = model_width // HEADS
+    attended = jnp.zeros((rows, model_width), jnp.float32)
+    for v in range(views):
+        slots = arrived[v].shape[0]
+        pick = jnp.where(place_ref[:, v : v + 1] == iota((rows, slots), 1), 1.0, 0.0)
+        attended += jnp.dot(
+            pick.astype(jnp.bfloat16), arrived[v][...], preferred_element_type=jnp.float32
+        )
+    attended = attended.reshape(rows // list_length, list_length, model_width)
+    residual = (states_ref[...][:, None, :] + attended).reshape(rows, model_width)
+    normed = layer_norm(residual).astype(jnp.bfloat16)
     projected = jnp.dot(
-        normed.reshape(track_rows * list_length, model_width),
-        w_temporal,
-        preferred_element_type=jnp.float32,
+        normed, w_temporal_ref[...], preferred_element_type=jnp.float32
     ).astype(jnp.bfloat16)
-    projected = projected.reshape(track_rows, list_length, 3, HEADS, head_feature_width)
-    per_head_queries = projected[:, :, 0]
-    per_head_keys = projected[:, :, 1]
-    per_head_values = projected[:, :, 2]
-    attention_scores = jnp.einsum(
-        "bqhd,bkhd->bhqk", per_head_queries, per_head_keys, preferred_element_type=jnp.float32
-    )
-    attention_scores = attention_scores * (
-        temporal_scale[None, :, None, None] * head_feature_width ** (-0.5)
-    )
-    positions = jnp.arange(list_length)
-    key_valid = positions[None, :] < counts[:, None]
-    attention_scores = jnp.where(key_valid[:, None, None, :], attention_scores, masked_score)
-    row_top = jnp.max(attention_scores, axis=-1, keepdims=True)
-    weights = jnp.exp(attention_scores - row_top)
-    probs = (weights / jnp.sum(weights, axis=-1, keepdims=True)).astype(jnp.bfloat16)
-    mixed_heads = jnp.einsum(
-        "bhqk,bkhd->bqhd", probs, per_head_values, preferred_element_type=jnp.float32
-    ).astype(jnp.bfloat16)
-    mixed_heads = mixed_heads.reshape(track_rows * list_length, model_width)
-    updated = residual_rows + jnp.dot(
-        mixed_heads, w_merge, preferred_element_type=jnp.float32
-    ).reshape(track_rows, list_length, model_width)
-    row_valid = key_valid.astype(jnp.float32)[:, :, None]
-    refined = (updated * row_valid).astype(jnp.bfloat16)
-    box_input = (layer_norm(updated) * box_gain).astype(jnp.bfloat16)
-    box_hidden = jax.nn.gelu(
-        jnp.dot(
-            box_input.reshape(track_rows * list_length, model_width),
-            w_hidden,
+    small = math.gcd(rows, 128)
+    row, column = iota((small, small), 0), iota((small, small), 1)
+    same = row // list_length == column // list_length
+    pieces = [(slice(low, low + small), head) for low in range(0, rows, small) for head in range(HEADS)]
+
+    def columns(array, here, block, head):
+        at = block * model_width + head * head_width
+        return array[here, at : at + head_width]
+
+    scores = []
+    for here, head in pieces:
+        score = lax.dot_general(
+            columns(projected, here, 0, head),
+            columns(projected, here, 1, head),
+            (((1,), (1,)), ((), ())),
             preferred_element_type=jnp.float32,
         )
-        + b_hidden
-    ).astype(jnp.bfloat16)
-    box_values = (
-        jnp.dot(box_hidden, w_box, preferred_element_type=jnp.float32).reshape(
-            track_rows, list_length, w_box.shape[1]
-        )
-        * row_valid
-    )
-    return (refined, box_values)
+        score = score * (scale_ref[head] * head_width ** (-0.5))
+        included = same & (column % list_length < key_counts_ref[:, here])
+        scores.append(jnp.where(included, score, masked_score))
+    scores = jnp.concatenate(scores, axis=0)
+    weights = jnp.exp(scores - jnp.max(scores, axis=1, keepdims=True))
+    probs = (weights / jnp.sum(weights, axis=1, keepdims=True)).astype(jnp.bfloat16)
+    for number, (here, head) in enumerate(pieces):
+        mixed_ref[here, head * head_width : (head + 1) * head_width] = jnp.dot(
+            probs[number * small : (number + 1) * small],
+            columns(projected, here, 2, head),
+            preferred_element_type=jnp.float32,
+        ).astype(jnp.bfloat16)
+    updated = residual + jnp.dot(
+        mixed_ref[...], w_merge_ref[...], preferred_element_type=jnp.float32
+    )
+    shown = jnp.where(iota((rows, 1), 0) % list_length < counts_ref[...], 1.0, 0.0)
+    refined_ref[...] = (updated * shown).astype(jnp.bfloat16)
+    box_input = (layer_norm(updated) * box_gain_ref[...]).astype(jnp.bfloat16)
+    hidden = jnp.dot(box_input, w_hidden_ref[...], preferred_element_type=jnp.float32)
+    hidden = hidden + b_hidden_ref[...]
+    cubic = hidden + 0.044715 * (hidden * hidden * hidden)
+    hidden = 0.5 * hidden * (1.0 + jnp.tanh(math.sqrt(2.0 / math.pi) * cubic))
+    boxes = jnp.dot(
+        hidden.astype(jnp.bfloat16), w_box_ref[...], preferred_element_type=jnp.float32
+    )
+    boxes_ref[...] = (boxes * shown).reshape(boxes_ref.shape)
+
+
+def track_rows(
+    states, places, counts, arrived, w_temporal, temporal_scale, w_merge, box_gain, w_hidden, b_hidden, w_box
+):
+    row_total = places.shape[0]
+    track_total, model_width = states.shape
+    list_length = row_total // track_total
+    tracks = math.gcd(TRACK_BLOCK, track_total)
+    rows = tracks * list_length
+    whole = lambda a: pl.BlockSpec(a.shape, lambda i: (0, 0))
+    by_row = lambda width, height=rows: pl.BlockSpec((height, width), lambda i: (i, 0))
+    row_counts = jnp.repeat(counts, list_length)
+    operands = [
+        temporal_scale,
+        states,
+        places,
+        row_counts.reshape(row_total, 1),
+        row_counts.reshape(1, row_total),
+        *arrived,
+        w_temporal,
+        w_merge,
+        box_gain.reshape(1, -1),
+        w_hidden,
+        b_hidden.reshape(1, -1),
+        w_box,
+    ]
+    specs = [
+        pl.BlockSpec(memory_space=pltpu.SMEM),
+        by_row(model_width, tracks),
+        by_row(places.shape[1]),
+        by_row(1),
+        pl.BlockSpec((1, rows), lambda i: (0, i)),
+    ] + [whole(a) for a in operands[5:]]
+    return pl.pallas_call(
+        lambda *refs: track_kernel(*refs, views=len(arrived), list_length=list_length),
+        grid=(row_total // rows,),
+        in_specs=specs,
+        out_specs=[
+            by_row(model_width),
+            pl.BlockSpec((tracks, list_length, w_box.shape[1]), lambda i: (i, 0, 0)),
+        ],
+        out_shape=[
+            jax.ShapeDtypeStruct((row_total, model_width), jnp.bfloat16),
+            jax.ShapeDtypeStruct((track_total, list_length, w_box.shape[1]), jnp.float32),
+        ],
+        scratch_shapes=[pltpu.VMEM((rows, model_width), jnp.bfloat16)],
+        name="track_rows",
+    )(*operands)
 
 
 def local(
@@ -431,20 +503,16 @@
     index = jnp.arange(row_local, dtype=jnp.int32)
     ahead = (flat[None, :] == flat[:, None]) & (index[None, :] < index[:, None])
     place = flat // local_views * capacity + jnp.sum(ahead.astype(jnp.int32), axis=1)
-    slots = device_count * capacity
-    attended = jnp.zeros((row_local, model_width), jnp.float32)
-    for view, arrived in enumerate(returned):
-        wanted = jnp.where((flat >= 0) & (flat % local_views == view), place, -1)
-        pick = (wanted[:, None] == jnp.arange(slots)[None, :]).astype(jnp.bfloat16)
-        attended += jnp.dot(
-            pick, arrived.reshape(slots, model_width), preferred_element_type=jnp.float32
-        )
-    attended = attended.reshape(track_local, list_length, model_width)
+    places = [
+        jnp.where((flat >= 0) & (flat % local_views == view), place, -1)
+        for view in range(len(returned))
+    ]
     states = layer_norm(track_embed.astype(jnp.float32)) * track_gain
-    return track_block(
+    refined, boxes = track_rows(
         states,
-        attended,
+        jnp.stack(places, axis=1),
         view_count,
+        [arrived.reshape(-1, model_width) for arrived in returned],
         w_temporal,
         temporal_scale,
         w_merge,
@@ -453,6 +521,10 @@
         b_hidden,
         w_box,
     )
+    return (
+        refined.reshape(track_local, list_length, model_width),
+        boxes,
+    )
 
 
 def solution(mesh):

time: 155 us -> 142 us (0.916)
  blocking collectives: 0 us -> 34 us
  waiting for transfers between devices: 67.7 us -> 42 us
  matrix products: 21.4 us -> 0 us
  Pallas kernels: 20.4 us -> 35 us
  starting transfers between devices: 27 us -> 16.2 us
  other arithmetic: 6.39 us -> 4.26 us
    all_to_all x0 -> x1, blocking collectives: none -> 34 us  [local(): lax.all_to_all(outbound.reshape(device_count, capacity, model_width), ('t...]
    ppermute x2, waiting for transfers between devices: 32 us -> 7.48 us  [from_behind(): return lax.ppermute(block, axis, route)]
    dot_general x6 -> x0, matrix products: 17.3 us -> none  [the longest x1 6.45 us: track_block(): jnp.dot(normed.reshape(track_rows * list_length, model_width), w_temporal...]
    pallas_call x0 -> x1, Pallas kernels: none -> 14.6 us  [track_rows(): pl.pallas_call(lambda *refs: track_kernel(*refs, views=len(arrived), list...]
    all_to_all x2 -> x1, starting transfers between devices: 13.8 us -> 3.81 us  [local(): lax.all_to_all(outbound.reshape(device_count, capacity, model_width), ('t...]
    sub x1 -> x0, matrix products: 4.13 us -> none  [track_block(): weights = jnp.exp(attention_scores - row_top)]
    another operation x0 -> x3, local copies, waits for them, and re-layouts: none -> 2.41 us  [the longest x1 0.88 us: track_rows(): row_counts.reshape(row_total, 1)]
    slice x1 -> x0, local copies, waits for them, and re-layouts: 2.28 us -> none  [track_block(): per_head_values = projected[:, :, 2]]
  transfers between devices with their start and end apart: 13 -> 12, of which waited for: 10 -> 9; matrix products, arithmetic and copies ran while one was open for 5% -> 6% of each run, Pallas kernels for 7% -> 7%
where the time goes in v1:
time: 142 us; the launch traced here: 141 us
  waiting for transfers between devices  42 us (30%)
  Pallas kernels  35 us (25%)
  blocking collectives  34 us (24%)
  starting transfers between devices  16.2 us (11%)
  local copies, waits for them, and re-layouts  9.18 us (6%)
  other arithmetic  4.26 us (3%)
    all_to_all x1, blocking collectives, local(): lax.all_to_all(outbound.reshape(device_count, capacity, model_width), ('t...  34 us
    all_to_all x1, waiting for transfers between devices, local(): lax.all_to_all(outbound.reshape(device_count, capacity, model_width), ('t...  21.2 us
    pallas_call x2, Pallas kernels, attend_view(): pl.pallas_call(lambda *refs: attend_kernel(*refs, row_block=row_block, co...  20.4 us
    pallas_call x1, Pallas kernels, track_rows(): pl.pallas_call(lambda *refs: track_kernel(*refs, views=len(arrived), list...  14.6 us
    ppermute x9, waiting for transfers between devices, exchange(): return lax.ppermute(block, axis, [(i, i ^ stride) for i in range(size)])  13.3 us
    ppermute x9, starting transfers between devices, exchange(): return lax.ppermute(block, axis, [(i, i ^ stride) for i in range(size)])  11.2 us
    ppermute x2, waiting for transfers between devices, from_behind(): return lax.ppermute(block, axis, route)  7.48 us
    unnamed x19, local copies, waits for them, and re-layouts  4.34 us
  transfers between devices with their start and end apart: 12, of which 9 were waited for; matrix products, arithmetic and copies ran while one was open for 6% of the time, Pallas kernels for 7%

profile of v1, /device:TPU:0, one launch (start us, length us, event | category | flops | bytes accessed | tf_op | source)
XLA Modules:
  0.0 141.4 jit_solution(16205878769190725978)
XLA Ops:
  0.6 0.8 fusion.21
  1.4 0.8 copy.42
  2.2 0.0 copy-start.3
  2.2 0.9 fusion.18
  3.1 3.1 %collective-permute-start = (bf16[32,1152]{1,0:T(8,128)(2,1)S(1)}, bf16[32,1152]{1,0:T(8,128)(2,1)S(1)}, u32[]{:S(2)}, u32[]{:S(2)}) collective-permute-start(bf16[32,1152]{1,0:T(8,128)(2,1)S(1)} %pad_maximum_fusion.5), channel_id=1, source_target_pairs={{0,8},{4,12},{8,0},{12,4},{16,24},{20,28},{24,16},{28,20},{1,9},{5... | collective-permute-start | bytes 221192 | tf_op jit(solution)/shard_map/ppermute | solution.py:46
  6.2 2.6 %collective-permute-start.1 = (bf16[32,1152]{1,0:T(8,128)(2,1)S(1)}, bf16[32,1152]{1,0:T(8,128)(2,1)S(1)}, u32[]{:S(2)}, u32[]{:S(2)}) collective-permute-start(bf16[32,1152]{1,0:T(8,128)(2,1)S(1)} %pad_maximum_fusion.5), channel_id=1, source_target_pairs={{0,16},{4,20},{8,24},{12,28},{16,0},{20,4},{24,8},{28,12},{1,17},{... | collective-permute-start | bytes 221192 | tf_op jit(solution)/shard_map/ppermute | solution.py:46
  8.8 0.0 collective-permute-start.2
  8.8 1.3 slice.26
  10.1 0.0 copy-done.3
  10.1 0.1 slice.27
  10.2 0.0 collective-permute-done
  10.2 3.8 %collective-permute-done.1 = bf16[32,1152]{1,0:T(8,128)(2,1)S(1)} collective-permute-done((bf16[32,1152]{1,0:T(8,128)(2,1)S(1)}, bf16[32,1152]{1,0:T(8,128)(2,1)S(1)}, u32[]{:S(2)}, u32[]{:S(2)}) %collective-permute-start.1) | collective-permute-done | bytes 73760 | tf_op jit(solution)/shard_map/ppermute | solution.py:46
  14.0 1.1 collective-permute-done.2
  15.1 1.6 %collective-permute-start.3 = (bf16[128,640]{1,0:T(8,128)(2,1)S(1)}, bf16[128,640]{1,0:T(8,128)(2,1)S(1)}, u32[]{:S(2)}, u32[]{:S(2)}) collective-permute-start(bf16[128,640]{1,0:T(8,128)(2,1)S(1)} %slice.28), channel_id=1, source_target_pairs={{0,4},{4,0},{8,12},{12,8},{16,20},{20,16},{24,28},{28,24},{1,5},{5... | collective-permute-start | bytes 491528 | tf_op jit(solution)/shard_map/ppermute | solution.py:46
  16.7 1.6 %collective-permute-start.6 = (bf16[128,512]{1,0:T(8,128)(2,1)S(1)}, bf16[128,512]{1,0:T(8,128)(2,1)S(1)}, u32[]{:S(2)}, u32[]{:S(2)}) collective-permute-start(bf16[128,512]{1,0:T(8,128)(2,1)S(1)} %slice.29), channel_id=1, source_target_pairs={{0,2},{1,3},{2,0},{3,1},{4,6},{5,7},{6,4},{7,5},{8,10},{9,11},{10,... | collective-permute-start | bytes 393224 | tf_op jit(solution)/shard_map/ppermute | solution.py:46
  18.3 2.2 %collective-permute-done.3 = bf16[128,640]{1,0:T(8,128)(2,1)S(1)} collective-permute-done((bf16[128,640]{1,0:T(8,128)(2,1)S(1)}, bf16[128,640]{1,0:T(8,128)(2,1)S(1)}, u32[]{:S(2)}, u32[]{:S(2)}) %collective-permute-start.3) | collective-permute-done | bytes 163872 | tf_op jit(solution)/shard_map/ppermute | solution.py:46
  20.5 1.6 %collective-permute-start.4 = (bf16[256,640]{1,0:T(8,128)(2,1)S(1)}, bf16[256,640]{1,0:T(8,128)(2,1)S(1)}, u32[]{:S(2)}, u32[]{:S(2)}) collective-permute-start(bf16[256,640]{1,0:T(8,128)(2,1)S(1)} %pad_maximum_fusion.2), channel_id=1, source_target_pairs={{0,2},{1,3},{2,0},{3,1},{4,6},{5,7},{6,4},{7,5},{8,10},{9,11},{10,... | collective-permute-start | bytes 983048 | tf_op jit(solution)/shard_map/ppermute | solution.py:46
  22.1 1.0 collective-permute-done.6
  23.1 0.7 collective-permute-start.7
  23.8 0.0 collective-permute-start.10
  23.8 1.1 collective-permute-start.9
  24.9 3.6 %collective-permute-done.4 = bf16[256,640]{1,0:T(8,128)(2,1)S(1)} collective-permute-done((bf16[256,640]{1,0:T(8,128)(2,1)S(1)}, bf16[256,640]{1,0:T(8,128)(2,1)S(1)}, u32[]{:S(2)}, u32[]{:S(2)}) %collective-permute-start.4) | collective-permute-done | bytes 327712 | tf_op jit(solution)/shard_map/ppermute | solution.py:46
  28.5 0.1 pad_maximum_fusion.refs_1_
  28.5 0.0 copy-start.2
  28.6 0.1 collective-permute-start.5
  28.6 0.9 collective-permute-done.7
  29.6 0.0 copy-start.4
  29.6 0.1 collective-permute-start.8
  29.7 0.6 pad_add_fusion.1.refs_0_
  30.3 0.1 fusion.16
  30.4 0.6 pad_maximum_fusion.6.refs_10_
  31.0 0.7 collective-permute-done.8.refs_4_
  31.7 0.0 collective-permute-done.5.refs_2_
  31.8 0.0 copy-done.2
  31.8 0.0 copy-done.4
  31.8 10.2 %attend_view.2 = bf16[512,1024]{1,0:T(8,128)(2,1)} custom-call(s32[2]{0:T(128)} %pad_add_fusion.1.refs_0_, bf16[512,640]{1,0:T(8,128)(2,1)} %copy-done.2, bf16[512,640]{1,0:T(8,128)(2,1)} %collective-permute-done.5.refs_2_, bf16[512,512]{1,0:T(8,128)(2,1)} %copy-done.4, bf16[512,512]{1,0:T(8,128)(2,1)} %collective-permute-done.8.refs_4_, ...), custom_call_target="tpu_custom_call" | custom-call | flops 4294967296 | bytes 8388608 | tf_op jit(solution)/shard_map/attend_view/pallas_call | solution.py:259
  41.9 0.6 pad_add_fusion.2.refs_0_
  42.5 0.0 collective-permute-done.10.refs_8_
  42.5 7.5 %collective-permute-done.9.refs_6_ = bf16[1,1,512,1024]{3,2,1,0:T(8,128)(2,1)} collective-permute-done((bf16[1,1,512,1024]{3,2,1,0:T(8,128)(2,1)S(1)}, bf16[1,1,512,1024]{3,2,1,0:T(8,128)(2,1)}, u32[]{:S(2)}, u32[]{:S(2)}) %collective-permute-start.9) | collective-permute-done | bytes 1048608 | tf_op jit(solution)/shard_map/ppermute | solution.py:21
  50.0 10.2 %attend_view.3 = bf16[512,1024]{1,0:T(8,128)(2,1)} custom-call(s32[2]{0:T(128)} %pad_add_fusion.2.refs_0_, bf16[512,640]{1,0:T(8,128)(2,1)} %copy-done.2, bf16[512,640]{1,0:T(8,128)(2,1)} %collective-permute-done.5.refs_2_, bf16[512,512]{1,0:T(8,128)(2,1)} %copy-done.4, bf16[512,512]{1,0:T(8,128)(2,1)} %collective-permute-done.8.refs_4_, ...), custom_call_target="tpu_custom_call" | custom-call | flops 4294967296 | bytes 8388608 | tf_op jit(solution)/shard_map/attend_view/pallas_call | solution.py:259
  60.2 34.0 %all_to_all.10 = bf16[32,16,1024]{2,1,0:T(8,128)(2,1)} all-to-all(bf16[32,16,1024]{2,1,0:T(8,128)(2,1)} %bitcast.14), channel_id=1, replica_groups=mesh['tm'=8,'trk'=4] {'tm','trk'}, dimensions={0} | all-to-all | bytes 2097152 | tf_op jit(solution)/shard_map/all_to_all | solution.py:493
  94.2 0.0 copy-start.7
  94.2 0.0 copy-start.5
  94.2 0.0 copy-start.1
  94.2 3.8 %all-to-all-start = ((bf16[32,16,1024]{2,1,0:T(8,128)(2,1)}), bf16[32,16,1024]{2,1,0:T(8,128)(2,1)S(1)}, u32[]{:S(2)}, u32[]{:S(2)}) async-start(bf16[32,16,1024]{2,1,0:T(8,128)(2,1)} %bitcast.4), calls=%async_computation | async-start | bytes 2097152 | tf_op jit(solution)/shard_map/all_to_all | solution.py:493
  98.0 0.1 reshape.232
  98.1 0.1 eq.44
  98.2 0.0 copy-done.7
  98.2 0.1 lt.47
  98.2 0.9 reshape_reshape.8.refs_3_
  99.1 0.7 reshape_reshape.7.refs_4_
  99.8 0.2 convert_reduce_fusion
  100.1 0.9 copy.46.refs_2_
  101.0 0.0 copy-done.5
  101.0 0.8 copy.48.refs_12_
  101.8 0.0 copy-done.1
  101.8 0.1 convert_reduce_fusion.1
  101.9 0.2 fusion.3
  102.1 0.0 copy-done.6
  102.1 0.7 fusion.4.refs_1_
  102.8 21.2 %all-to-all-done = bf16[32,16,1024]{2,1,0:T(8,128)(2,1)S(1)} async-done(((bf16[32,16,1024]{2,1,0:T(8,128)(2,1)}), bf16[32,16,1024]{2,1,0:T(8,128)(2,1)S(1)}, u32[]{:S(2)}, u32[]{:S(2)}) %all-to-all-start) | async-done | bytes 1048608 | tf_op jit(solution)/shard_map/all_to_all | solution.py:493
  124.0 1.0 copy-done
  125.0 14.6 %track_rows.1 = (bf16[512,1024]{1,0:T(8,128)(2,1)}, f32[32,16,10]{2,1,0:T(8,128)}) custom-call(f32[8]{0:T(128)} %refs_0_.1, f32[32,1024]{1,0:T(8,128)} %fusion.4.refs_1_, s32[512,2]{1,0:T(8,128)} %copy.46.refs_2_, s32[512,1]{1,0:T(8,128)} %reshape_reshape.8.refs_3_, s32[1,512]{1,0:T(1,128)} %reshape_reshape.7.refs_4_, bf16[512,1024]{1,0:T(8,128)(2,1)} %bitcast.13, ...), custom_call_target="tpu_custom_call" | custom-call | tf_op jit(solution)/shard_map/track_rows/pallas_call | solution.py:406
  139.6 1.8 %copy.49 = f32[32,16,10]{0,1,2:T(8,128)} copy(f32[32,16,10]{2,1,0:T(8,128)} %get-tuple-element.25) | data formatting | bytes 40960
  (16 shorter events, 0.2 us)
Async XLA Ops:
  2.2 7.9 %copy-start.3 = (bf16[1,2,512,1024]{3,2,1,0:T(8,128)(2,1)S(1)}, bf16[1,2,512,1024]{3,2,1,0:T(8,128)(2,1)}, u32[]{:S(2)}) copy-start(bf16[1,2,512,1024]{3,2,1,0:T(8,128)(2,1)} %refs_7_.4) | copy-start | bytes 6291460
  3.1 7.1 %collective-permute-start = (bf16[32,1152]{1,0:T(8,128)(2,1)S(1)}, bf16[32,1152]{1,0:T(8,128)(2,1)S(1)}, u32[]{:S(2)}, u32[]{:S(2)}) collective-permute-start(bf16[32,1152]{1,0:T(8,128)(2,1)S(1)} %pad_maximum_fusion.5), channel_id=1, source_target_pairs={{0,8},{4,12},{8,0},{12,4},{16,24},{20,28},{24,16},{28,20},{1,9},{5... | collective-permute-start | bytes 221192 | tf_op jit(solution)/shard_map/ppermute | solution.py:46
  6.2 7.8 %collective-permute-start.1 = (bf16[32,1152]{1,0:T(8,128)(2,1)S(1)}, bf16[32,1152]{1,0:T(8,128)(2,1)S(1)}, u32[]{:S(2)}, u32[]{:S(2)}) collective-permute-start(bf16[32,1152]{1,0:T(8,128)(2,1)S(1)} %pad_maximum_fusion.5), channel_id=1, source_target_pairs={{0,16},{4,20},{8,24},{12,28},{16,0},{20,4},{24,8},{28,12},{1,17},{... | collective-permute-start | bytes 221192 | tf_op jit(solution)/shard_map/ppermute | solution.py:46
  8.8 6.3 %collective-permute-start.2 = (bf16[32,1152]{1,0:T(8,128)(2,1)S(1)}, bf16[32,1152]{1,0:T(8,128)(2,1)S(1)}, u32[]{:S(2)}, u32[]{:S(2)}) collective-permute-start(bf16[32,1152]{1,0:T(8,128)(2,1)S(1)} %pad_maximum_fusion.5), channel_id=1, source_target_pairs={{0,24},{4,28},{8,16},{12,20},{16,8},{20,12},{24,0},{28,4},{1,25},{... | collective-permute-start | bytes 221192 | tf_op jit(solution)/shard_map/ppermute | solution.py:46
  15.1 5.4 %collective-permute-start.3 = (bf16[128,640]{1,0:T(8,128)(2,1)S(1)}, bf16[128,640]{1,0:T(8,128)(2,1)S(1)}, u32[]{:S(2)}, u32[]{:S(2)}) collective-permute-start(bf16[128,640]{1,0:T(8,128)(2,1)S(1)} %slice.28), channel_id=1, source_target_pairs={{0,4},{4,0},{8,12},{12,8},{16,20},{20,16},{24,28},{28,24},{1,5},{5... | collective-permute-start | bytes 491528 | tf_op jit(solution)/shard_map/ppermute | solution.py:46
  16.7 6.4 %collective-permute-start.6 = (bf16[128,512]{1,0:T(8,128)(2,1)S(1)}, bf16[128,512]{1,0:T(8,128)(2,1)S(1)}, u32[]{:S(2)}, u32[]{:S(2)}) collective-permute-start(bf16[128,512]{1,0:T(8,128)(2,1)S(1)} %slice.29), channel_id=1, source_target_pairs={{0,2},{1,3},{2,0},{3,1},{4,6},{5,7},{6,4},{7,5},{8,10},{9,11},{10,... | collective-permute-start | bytes 393224 | tf_op jit(solution)/shard_map/ppermute | solution.py:46
  20.5 8.0 %collective-permute-start.4 = (bf16[256,640]{1,0:T(8,128)(2,1)S(1)}, bf16[256,640]{1,0:T(8,128)(2,1)S(1)}, u32[]{:S(2)}, u32[]{:S(2)}) collective-permute-start(bf16[256,640]{1,0:T(8,128)(2,1)S(1)} %pad_maximum_fusion.2), channel_id=1, source_target_pairs={{0,2},{1,3},{2,0},{3,1},{4,6},{5,7},{6,4},{7,5},{8,10},{9,11},{10,... | collective-permute-start | bytes 983048 | tf_op jit(solution)/shard_map/ppermute | solution.py:46
  23.1 6.4 %collective-permute-start.7 = (bf16[256,512]{1,0:T(8,128)(2,1)S(1)}, bf16[256,512]{1,0:T(8,128)(2,1)S(1)}, u32[]{:S(2)}, u32[]{:S(2)}) collective-permute-start(bf16[256,512]{1,0:T(8,128)(2,1)S(1)} %pad_maximum_fusion.4), channel_id=1, source_target_pairs={{0,4},{4,0},{8,12},{12,8},{16,20},{20,16},{24,28},{28,24},{1,5},{5... | collective-permute-start | bytes 786440 | tf_op jit(solution)/shard_map/ppermute | solution.py:46
  23.8 18.7 %collective-permute-start.10 = (bf16[1,1,512,1024]{3,2,1,0:T(8,128)(2,1)S(1)}, bf16[1,1,512,1024]{3,2,1,0:T(8,128)(2,1)}, u32[]{:S(2)}, u32[]{:S(2)}) collective-permute-start(bf16[1,1,512,1024]{3,2,1,0:T(8,128)(2,1)S(1)} %slice.27), channel_id=1, source_target_pairs={{1,0},{2,1},{3,2},{0,3},{5,4},{6,5},{7,6},{4,7},{9,8},{10,9},{11,1... | collective-permute-start | bytes 3145736 | tf_op jit(solution)/shard_map/ppermute | solution.py:21
  23.8 26.2 %collective-permute-start.9 = (bf16[1,1,512,1024]{3,2,1,0:T(8,128)(2,1)S(1)}, bf16[1,1,512,1024]{3,2,1,0:T(8,128)(2,1)}, u32[]{:S(2)}, u32[]{:S(2)}) collective-permute-start(bf16[1,1,512,1024]{3,2,1,0:T(8,128)(2,1)S(1)} %slice.26), channel_id=1, source_target_pairs={{1,0},{2,1},{3,2},{0,3},{5,4},{6,5},{7,6},{4,7},{9,8},{10,9},{11,1... | collective-permute-start | bytes 3145736 | tf_op jit(solution)/shard_map/ppermute | solution.py:21
  28.5 3.2 %copy-start.2 = (bf16[512,640]{1,0:T(8,128)(2,1)}, bf16[512,640]{1,0:T(8,128)(2,1)S(1)}, u32[]{:S(2)}) copy-start(bf16[512,640]{1,0:T(8,128)(2,1)S(1)} %pad_maximum_fusion.refs_1_) | copy-start | bytes 1966084
  28.6 3.2 %collective-permute-start.5 = (bf16[512,640]{1,0:T(8,128)(2,1)S(1)}, bf16[512,640]{1,0:T(8,128)(2,1)}, u32[]{:S(2)}, u32[]{:S(2)}) collective-permute-start(bf16[512,640]{1,0:T(8,128)(2,1)S(1)} %pad_maximum_fusion.refs_1_), channel_id=1, source_target_pairs={{0,1},{1,0},{2,3},{3,2},{4,5},{5,4},{6,7},{7,6},{8,9},{9,8},{10,11... | collective-permute-start | bytes 1966088 | tf_op jit(solution)/shard_map/ppermute | solution.py:46
  29.6 2.1 %copy-start.4 = (bf16[512,512]{1,0:T(8,128)(2,1)}, bf16[512,512]{1,0:T(8,128)(2,1)S(1)}, u32[]{:S(2)}) copy-start(bf16[512,512]{1,0:T(8,128)(2,1)S(1)} %pad_maximum_fusion.1.refs_3_) | copy-start | bytes 1572868
  29.6 2.1 %collective-permute-start.8 = (bf16[512,512]{1,0:T(8,128)(2,1)S(1)}, bf16[512,512]{1,0:T(8,128)(2,1)}, u32[]{:S(2)}, u32[]{:S(2)}) collective-permute-start(bf16[512,512]{1,0:T(8,128)(2,1)S(1)} %pad_maximum_fusion.1.refs_3_), channel_id=1, source_target_pairs={{0,1},{1,0},{2,3},{3,2},{4,5},{5,4},{6,7},{7,6},{8,9},{9,8},{10,11... | collective-permute-start | bytes 1572872 | tf_op jit(solution)/shard_map/ppermute | solution.py:46
  94.2 4.0 %copy-start.7 = (s32[32]{0:T(128)S(1)}, s32[32]{0:T(128)}, u32[]{:S(2)}) copy-start(s32[32]{0:T(128)} %param.15) | copy-start | bytes 388
  94.2 6.8 %copy-start.5 = (bf16[512,10]{0,1:T(8,128)(2,1)S(1)}, bf16[512,10]{0,1:T(8,128)(2,1)}, u32[]{:S(2)}) copy-start(bf16[512,10]{0,1:T(8,128)(2,1)} %param.25) | copy-start | bytes 30724
  94.2 7.6 %copy-start.1 = (bf16[32,1024]{1,0:T(8,128)(2,1)S(1)}, bf16[32,1024]{1,0:T(8,128)(2,1)}, u32[]{:S(2)}) copy-start(bf16[32,1024]{1,0:T(8,128)(2,1)} %param.13) | copy-start | bytes 196612
  94.2 7.9 %copy-start.6 = (f32[1024]{0:T(1024)S(1)}, f32[1024]{0:T(1024)}, u32[]{:S(2)}) copy-start(f32[1024]{0:T(1024)} %param.18) | copy-start | bytes 12292
  94.2 29.8 %all-to-all-start = ((bf16[32,16,1024]{2,1,0:T(8,128)(2,1)}), bf16[32,16,1024]{2,1,0:T(8,128)(2,1)S(1)}, u32[]{:S(2)}, u32[]{:S(2)}) async-start(bf16[32,16,1024]{2,1,0:T(8,128)(2,1)} %bitcast.4), calls=%async_computation | async-start | bytes 2097152 | tf_op jit(solution)/shard_map/all_to_all | solution.py:493
  124.0 1.0 copy-start
